TPU v7x, 32 devices: a whole 2x2x4 slice. The times are simulated.
32 devices in a mesh: rep: 4 (over x, core), row: 2 (over y), col: 4 (over z).
Axes of the slice: x: 2, y: 2, z: 4, core: 2. Of those that a mesh axis runs over, the one named last changes fastest.
Arguments:
- spin_init: bfloat16 [256, 8192], P('rep', 'row'), may hold values from -1 to 1, as said below
- couplings: bfloat16 [2, 4, 1024, 8192], P(None, 'col', None, 'row'), may hold values from -1 to 1, as said below
- flip_noise: float32 [10, 256, 8192], P(None, 'rep', 'row'), may hold values from 0 to 17, as said below
- colors: int32 [8192], P('row'), may hold values 0 or 1
- beta_steps: int32 [256], replicated, may hold values from 96 to 1024
- partners: int32 [256], replicated, may hold values from 0 to 255, as said below
- swap_noise: float32 [256], replicated, may hold values from 0 to 17, as said below
Outputs:
- spins_out: bfloat16 [256, 8192], P('rep', 'row')
- energies: float32 [256], P('rep')
Inputs may be any that keep to these rules, and one draw needn't show every extreme that they name: `spin_init`: every entry is -1 or +1. `couplings`: the 8192 x 8192 matrix is symmetric, zero on its diagonal, and every other entry is -1 or +1. `flip_noise`: independent exponential variates of mean one. `swap_noise`: independent exponential variates of mean one. Pairs slots: partners[partners[r]] = r and partners[r] != r for every slot.
All inputs are finite; a program needn't handle non-finite values. No bound on the sum of `colors` on one device may be relied on, other than what follows from the above.
Results may differ from a plain program's by a relative error of at most 0.001.
Values may be sent and summed in bfloat16 or wider, within the bound.
A program may use at most 64 MiB of HBM per device.

v0:
```python
import math
import jax
import jax.numpy as jnp
from jax import lax
from jax.sharding import PartitionSpec as P

N = 8192
SWEEPS = 10


def metropolis(spin_state, fields, parity, color_part, noise_part, beta_col):
    values = spin_state.astype(jnp.float32)
    energy_cost = beta_col * (values * fields) * (1.0 / 16384.0)
    flipped = (color_part == parity)[None, :] & (energy_cost < noise_part)
    return jnp.where(flipped, -values, values).astype(jnp.bfloat16)


def partial_fields(strided, coupling_block):
    return jnp.dot(strided, coupling_block, preferred_element_type=jnp.float32)


def per_device(spin_init, couplings, flip_noise, colors, beta_steps, partners, swap_noise):
    rep_dev, row_width = spin_init.shape
    col_count = lax.axis_size("col")
    col_index = lax.axis_index("col")
    rep_index = lax.axis_index("rep")
    piece_size = row_width // col_count
    coupling_block = couplings.reshape(-1, row_width)
    beta_col = lax.dynamic_slice_in_dim(beta_steps, rep_index * rep_dev, rep_dev).astype(
        jnp.float32
    )[:, None]
    color_part = lax.dynamic_slice_in_dim(colors, col_index * piece_size, piece_size)
    noise_part = lax.dynamic_slice_in_dim(flip_noise, col_index * piece_size, piece_size, 2)

    def strided_of(spin_state):
        return lax.all_gather(spin_state, "row", axis=1, tiled=True)

    def one_sweep(step_index, spin_state):
        terms = partial_fields(strided_of(spin_state), coupling_block)
        fields = lax.psum_scatter(terms, "col", scatter_dimension=1, tiled=True)
        return metropolis(
            spin_state, fields, step_index % 2, color_part, noise_part[step_index], beta_col
        )

    start_pieces = lax.dynamic_slice_in_dim(spin_init, col_index * piece_size, piece_size, 1)
    final_pieces = lax.fori_loop(0, SWEEPS, one_sweep, start_pieces)
    strided = strided_of(final_pieces)
    final_rows = lax.all_gather(final_pieces, "col", axis=1, tiled=True)
    every_spins = lax.all_gather(final_rows, "rep", axis=0, tiled=True)
    final_partial = partial_fields(strided, coupling_block)
    row_values = final_rows.astype(jnp.float32)
    final_local = lax.psum(final_partial, "col")
    total_sum = lax.psum(jnp.sum(row_values * final_local, axis=1), "row")
    energy = -0.5 * total_sum
    every_energy = lax.all_gather(energy, "rep", axis=0, tiled=True)
    slot_ids = rep_index * rep_dev + jnp.arange(rep_dev, dtype=jnp.int32)
    mate_ids = lax.dynamic_slice_in_dim(partners, rep_index * rep_dev, rep_dev)
    all_betas = beta_steps.astype(jnp.float32)
    mate_energy = every_energy[mate_ids]
    swap_gain = (
        (beta_col[:, 0] - all_betas[mate_ids])
        * (energy - mate_energy)
        * (1.0 / (64.0 * N * math.sqrt(N)))
    )
    accept = swap_gain + swap_noise[jnp.minimum(slot_ids, mate_ids)] > 0.0
    spins_out = jnp.where(accept[:, None], every_spins[mate_ids], final_rows)
    energies = jnp.where(accept, mate_energy, energy) * (1.0 / (N * math.sqrt(N)))
    return (spins_out, energies)


def solution(mesh):
    in_specs = (
        P("rep", "row"),
        P(None, "col", None, "row"),
        P(None, "rep", "row"),
        P("row"),
        P(),
        P(),
        P(),
    )
    out_specs = (P("rep", "row"), P("rep"))
    return jax.shard_map(
        per_device, mesh=mesh, in_specs=in_specs, out_specs=out_specs, check_vma=False
    )
```

profile of v0, /device:TPU:0, one launch (start us, length us, event | category | flops | bytes accessed | tf_op | source)
XLA Modules:
  0.0 540.9 jit_solution(17251068194962414624)
XLA Ops:
  8.0 1.0 copy-done
  9.1 0.7 dynamic_slice.28
  9.8 1.9 constant_dynamic-slice_fusion
  11.7 0.8 convert_bitcast_fusion
  12.4 431.6 %while.15 = (s32[]{:T(128)}, bf16[64,1024]{1,0:T(8,128)(2,1)S(1)}, s32[1024]{0:T(1024)S(1)}, f32[64,1]{0,1:T(1,128)S(1)}, bf16[2048,4096]{1,0:T(8,128)(2,1)}, /*...) while((s32[]{:T(128)}, bf16[64,1024]{1,0:T(8,128)(2,1)S(1)}, s32[1024]{0:T(1024)S(1)}, ...), condition=%wide.region_2.3_spmd, body=%wide.region_0.2_spmd.sunk | while | flops 1074332672 | bytes 23206348 | solution.py:46
  12.4 7.1 %all_gather.27 = bf16[64,2048]{1,0:T(8,128)(2,1)S(1)} all-gather(bf16[64,1024]{1,0:T(8,128)(2,1)S(1)} %get-tuple-element.221), channel_id=1, replica_groups=mesh['rep'=4,'row'=2,'col'=4] {'row'}, dimensions={1}, use_global_device_ids=true | all-gather | bytes 393216 | tf_op jit(solution)/shard_map/while/body/eval_jaxpr/all_gather | solution.py:36
  19.6 9.8 %fusion.17 = f32[64,4096]{1,0:T(8,128)} fusion(bf16[64,2048]{1,0:T(8,128)(2,1)S(1)} %all_gather.27, bf16[2048,4096]{1,0:T(8,128)(2,1)} %get-tuple-element.233), kind=kOutput, calls=%fused_computation.24.clone.1 | convolution fusion | flops 1073741824 | bytes 18087936 | tf_op jit(solution)/shard_map/while/body/eval_jaxpr/dot_general | solution.py:19
  29.4 28.9 %reduce-scatter.2.cloned.1.call-done = f32[64,1024]{1,0:T(8,128)} async-done(((f32[64,4096]{1,0:T(8,128)}), f32[64,1024]{1,0:T(8,128)}) %reduce-scatter.2.cloned.1.call-update) | async-done | bytes 262160 | tf_op jit(solution)/shard_map/while/body/eval_jaxpr/reduce_scatter | solution.py:40
  58.3 1.1 fusion.18
  59.4 5.6 %all_gather.27 = bf16[64,2048]{1,0:T(8,128)(2,1)S(1)} all-gather(bf16[64,1024]{1,0:T(8,128)(2,1)S(1)} %get-tuple-element.221), channel_id=1, replica_groups=mesh['rep'=4,'row'=2,'col'=4] {'row'}, dimensions={1}, use_global_device_ids=true | all-gather | bytes 393216 | tf_op jit(solution)/shard_map/while/body/eval_jaxpr/all_gather | solution.py:36
  65.1 9.8 %fusion.17 = f32[64,4096]{1,0:T(8,128)} fusion(bf16[64,2048]{1,0:T(8,128)(2,1)S(1)} %all_gather.27, bf16[2048,4096]{1,0:T(8,128)(2,1)} %get-tuple-element.233), kind=kOutput, calls=%fused_computation.24.clone.1 | convolution fusion | flops 1073741824 | bytes 18087936 | tf_op jit(solution)/shard_map/while/body/eval_jaxpr/dot_general | solution.py:19
  74.9 26.1 %reduce-scatter.2.cloned.1.call-done = f32[64,1024]{1,0:T(8,128)} async-done(((f32[64,4096]{1,0:T(8,128)}), f32[64,1024]{1,0:T(8,128)}) %reduce-scatter.2.cloned.1.call-update) | async-done | bytes 262160 | tf_op jit(solution)/shard_map/while/body/eval_jaxpr/reduce_scatter | solution.py:40
  101.0 1.1 fusion.18
  102.1 0.0 reduce-scatter.2.cloned.1.call-start
  102.2 5.6 %all_gather.27 = bf16[64,2048]{1,0:T(8,128)(2,1)S(1)} all-gather(bf16[64,1024]{1,0:T(8,128)(2,1)S(1)} %get-tuple-element.221), channel_id=1, replica_groups=mesh['rep'=4,'row'=2,'col'=4] {'row'}, dimensions={1}, use_global_device_ids=true | all-gather | bytes 393216 | tf_op jit(solution)/shard_map/while/body/eval_jaxpr/all_gather | solution.py:36
  107.8 9.8 %fusion.17 = f32[64,4096]{1,0:T(8,128)} fusion(bf16[64,2048]{1,0:T(8,128)(2,1)S(1)} %all_gather.27, bf16[2048,4096]{1,0:T(8,128)(2,1)} %get-tuple-element.233), kind=kOutput, calls=%fused_computation.24.clone.1 | convolution fusion | flops 1073741824 | bytes 18087936 | tf_op jit(solution)/shard_map/while/body/eval_jaxpr/dot_general | solution.py:19
  117.6 26.1 %reduce-scatter.2.cloned.1.call-done = f32[64,1024]{1,0:T(8,128)} async-done(((f32[64,4096]{1,0:T(8,128)}), f32[64,1024]{1,0:T(8,128)}) %reduce-scatter.2.cloned.1.call-update) | async-done | bytes 262160 | tf_op jit(solution)/shard_map/while/body/eval_jaxpr/reduce_scatter | solution.py:40
  143.8 1.1 fusion.18
  144.9 5.6 %all_gather.27 = bf16[64,2048]{1,0:T(8,128)(2,1)S(1)} all-gather(bf16[64,1024]{1,0:T(8,128)(2,1)S(1)} %get-tuple-element.221), channel_id=1, replica_groups=mesh['rep'=4,'row'=2,'col'=4] {'row'}, dimensions={1}, use_global_device_ids=true | all-gather | bytes 393216 | tf_op jit(solution)/shard_map/while/body/eval_jaxpr/all_gather | solution.py:36
  150.5 9.8 %fusion.17 = f32[64,4096]{1,0:T(8,128)} fusion(bf16[64,2048]{1,0:T(8,128)(2,1)S(1)} %all_gather.27, bf16[2048,4096]{1,0:T(8,128)(2,1)} %get-tuple-element.233), kind=kOutput, calls=%fused_computation.24.clone.1 | convolution fusion | flops 1073741824 | bytes 18087936 | tf_op jit(solution)/shard_map/while/body/eval_jaxpr/dot_general | solution.py:19
  160.4 26.2 %reduce-scatter.2.cloned.1.call-done = f32[64,1024]{1,0:T(8,128)} async-done(((f32[64,4096]{1,0:T(8,128)}), f32[64,1024]{1,0:T(8,128)}) %reduce-scatter.2.cloned.1.call-update) | async-done | bytes 262160 | tf_op jit(solution)/shard_map/while/body/eval_jaxpr/reduce_scatter | solution.py:40
  186.5 1.1 fusion.18
  187.7 5.6 %all_gather.27 = bf16[64,2048]{1,0:T(8,128)(2,1)S(1)} all-gather(bf16[64,1024]{1,0:T(8,128)(2,1)S(1)} %get-tuple-element.221), channel_id=1, replica_groups=mesh['rep'=4,'row'=2,'col'=4] {'row'}, dimensions={1}, use_global_device_ids=true | all-gather | bytes 393216 | tf_op jit(solution)/shard_map/while/body/eval_jaxpr/all_gather | solution.py:36
  193.3 9.8 %fusion.17 = f32[64,4096]{1,0:T(8,128)} fusion(bf16[64,2048]{1,0:T(8,128)(2,1)S(1)} %all_gather.27, bf16[2048,4096]{1,0:T(8,128)(2,1)} %get-tuple-element.233), kind=kOutput, calls=%fused_computation.24.clone.1 | convolution fusion | flops 1073741824 | bytes 18087936 | tf_op jit(solution)/shard_map/while/body/eval_jaxpr/dot_general | solution.py:19
  203.1 26.1 %reduce-scatter.2.cloned.1.call-done = f32[64,1024]{1,0:T(8,128)} async-done(((f32[64,4096]{1,0:T(8,128)}), f32[64,1024]{1,0:T(8,128)}) %reduce-scatter.2.cloned.1.call-update) | async-done | bytes 262160 | tf_op jit(solution)/shard_map/while/body/eval_jaxpr/reduce_scatter | solution.py:40
  229.2 1.1 fusion.18
  230.4 5.6 %all_gather.27 = bf16[64,2048]{1,0:T(8,128)(2,1)S(1)} all-gather(bf16[64,1024]{1,0:T(8,128)(2,1)S(1)} %get-tuple-element.221), channel_id=1, replica_groups=mesh['rep'=4,'row'=2,'col'=4] {'row'}, dimensions={1}, use_global_device_ids=true | all-gather | bytes 393216 | tf_op jit(solution)/shard_map/while/body/eval_jaxpr/all_gather | solution.py:36
  236.0 9.8 %fusion.17 = f32[64,4096]{1,0:T(8,128)} fusion(bf16[64,2048]{1,0:T(8,128)(2,1)S(1)} %all_gather.27, bf16[2048,4096]{1,0:T(8,128)(2,1)} %get-tuple-element.233), kind=kOutput, calls=%fused_computation.24.clone.1 | convolution fusion | flops 1073741824 | bytes 18087936 | tf_op jit(solution)/shard_map/while/body/eval_jaxpr/dot_general | solution.py:19
  245.8 26.1 %reduce-scatter.2.cloned.1.call-done = f32[64,1024]{1,0:T(8,128)} async-done(((f32[64,4096]{1,0:T(8,128)}), f32[64,1024]{1,0:T(8,128)}) %reduce-scatter.2.cloned.1.call-update) | async-done | bytes 262160 | tf_op jit(solution)/shard_map/while/body/eval_jaxpr/reduce_scatter | solution.py:40
  272.0 1.1 fusion.18
  273.1 5.6 %all_gather.27 = bf16[64,2048]{1,0:T(8,128)(2,1)S(1)} all-gather(bf16[64,1024]{1,0:T(8,128)(2,1)S(1)} %get-tuple-element.221), channel_id=1, replica_groups=mesh['rep'=4,'row'=2,'col'=4] {'row'}, dimensions={1}, use_global_device_ids=true | all-gather | bytes 393216 | tf_op jit(solution)/shard_map/while/body/eval_jaxpr/all_gather | solution.py:36
  278.8 9.8 %fusion.17 = f32[64,4096]{1,0:T(8,128)} fusion(bf16[64,2048]{1,0:T(8,128)(2,1)S(1)} %all_gather.27, bf16[2048,4096]{1,0:T(8,128)(2,1)} %get-tuple-element.233), kind=kOutput, calls=%fused_computation.24.clone.1 | convolution fusion | flops 1073741824 | bytes 18087936 | tf_op jit(solution)/shard_map/while/body/eval_jaxpr/dot_general | solution.py:19
  288.6 26.1 %reduce-scatter.2.cloned.1.call-done = f32[64,1024]{1,0:T(8,128)} async-done(((f32[64,4096]{1,0:T(8,128)}), f32[64,1024]{1,0:T(8,128)}) %reduce-scatter.2.cloned.1.call-update) | async-done | bytes 262160 | tf_op jit(solution)/shard_map/while/body/eval_jaxpr/reduce_scatter | solution.py:40
  314.7 1.1 fusion.18
  315.8 0.0 reduce-scatter.2.cloned.1.call-start
  315.9 5.6 %all_gather.27 = bf16[64,2048]{1,0:T(8,128)(2,1)S(1)} all-gather(bf16[64,1024]{1,0:T(8,128)(2,1)S(1)} %get-tuple-element.221), channel_id=1, replica_groups=mesh['rep'=4,'row'=2,'col'=4] {'row'}, dimensions={1}, use_global_device_ids=true | all-gather | bytes 393216 | tf_op jit(solution)/shard_map/while/body/eval_jaxpr/all_gather | solution.py:36
  321.5 9.8 %fusion.17 = f32[64,4096]{1,0:T(8,128)} fusion(bf16[64,2048]{1,0:T(8,128)(2,1)S(1)} %all_gather.27, bf16[2048,4096]{1,0:T(8,128)(2,1)} %get-tuple-element.233), kind=kOutput, calls=%fused_computation.24.clone.1 | convolution fusion | flops 1073741824 | bytes 18087936 | tf_op jit(solution)/shard_map/while/body/eval_jaxpr/dot_general | solution.py:19
  331.3 26.1 %reduce-scatter.2.cloned.1.call-done = f32[64,1024]{1,0:T(8,128)} async-done(((f32[64,4096]{1,0:T(8,128)}), f32[64,1024]{1,0:T(8,128)}) %reduce-scatter.2.cloned.1.call-update) | async-done | bytes 262160 | tf_op jit(solution)/shard_map/while/body/eval_jaxpr/reduce_scatter | solution.py:40
  357.5 1.1 fusion.18
  358.6 5.6 %all_gather.27 = bf16[64,2048]{1,0:T(8,128)(2,1)S(1)} all-gather(bf16[64,1024]{1,0:T(8,128)(2,1)S(1)} %get-tuple-element.221), channel_id=1, replica_groups=mesh['rep'=4,'row'=2,'col'=4] {'row'}, dimensions={1}, use_global_device_ids=true | all-gather | bytes 393216 | tf_op jit(solution)/shard_map/while/body/eval_jaxpr/all_gather | solution.py:36
  364.3 9.8 %fusion.17 = f32[64,4096]{1,0:T(8,128)} fusion(bf16[64,2048]{1,0:T(8,128)(2,1)S(1)} %all_gather.27, bf16[2048,4096]{1,0:T(8,128)(2,1)} %get-tuple-element.233), kind=kOutput, calls=%fused_computation.24.clone.1 | convolution fusion | flops 1073741824 | bytes 18087936 | tf_op jit(solution)/shard_map/while/body/eval_jaxpr/dot_general | solution.py:19
  374.1 26.1 %reduce-scatter.2.cloned.1.call-done = f32[64,1024]{1,0:T(8,128)} async-done(((f32[64,4096]{1,0:T(8,128)}), f32[64,1024]{1,0:T(8,128)}) %reduce-scatter.2.cloned.1.call-update) | async-done | bytes 262160 | tf_op jit(solution)/shard_map/while/body/eval_jaxpr/reduce_scatter | solution.py:40
  400.2 1.1 fusion.18
  401.4 5.6 %all_gather.27 = bf16[64,2048]{1,0:T(8,128)(2,1)S(1)} all-gather(bf16[64,1024]{1,0:T(8,128)(2,1)S(1)} %get-tuple-element.221), channel_id=1, replica_groups=mesh['rep'=4,'row'=2,'col'=4] {'row'}, dimensions={1}, use_global_device_ids=true | all-gather | bytes 393216 | tf_op jit(solution)/shard_map/while/body/eval_jaxpr/all_gather | solution.py:36
  407.0 9.8 %fusion.17 = f32[64,4096]{1,0:T(8,128)} fusion(bf16[64,2048]{1,0:T(8,128)(2,1)S(1)} %all_gather.27, bf16[2048,4096]{1,0:T(8,128)(2,1)} %get-tuple-element.233), kind=kOutput, calls=%fused_computation.24.clone.1 | convolution fusion | flops 1073741824 | bytes 18087936 | tf_op jit(solution)/shard_map/while/body/eval_jaxpr/dot_general | solution.py:19
  416.8 26.1 %reduce-scatter.2.cloned.1.call-done = f32[64,1024]{1,0:T(8,128)} async-done(((f32[64,4096]{1,0:T(8,128)}), f32[64,1024]{1,0:T(8,128)}) %reduce-scatter.2.cloned.1.call-update) | async-done | bytes 262160 | tf_op jit(solution)/shard_map/while/body/eval_jaxpr/reduce_scatter | solution.py:40
  443.0 1.1 fusion.18
  444.1 0.0 all-reduce.3.cloned.1.call-start
  444.2 5.6 %all_gather.23 = bf16[64,2048]{1,0:T(8,128)(2,1)S(1)} all-gather(bf16[64,1024]{1,0:T(8,128)(2,1)S(1)} %get-tuple-element.157), channel_id=1, replica_groups=mesh['rep'=4,'row'=2,'col'=4] {'row'}, dimensions={1}, use_global_device_ids=true | all-gather | bytes 393216 | tf_op jit(solution)/shard_map/all_gather | solution.py:36
  449.8 9.8 %fusion.6 = f32[64,4096]{1,0:T(8,128)} fusion(bf16[64,2048]{1,0:T(8,128)(2,1)S(1)} %all_gather.23, bf16[2048,4096]{1,0:T(8,128)(2,1)} %get-tuple-element.241), kind=kOutput, calls=%fused_computation.25 | convolution fusion | flops 1073741824 | bytes 18087936 | tf_op jit(solution)/shard_map/dot_general | solution.py:19
  459.7 20.4 %all_gather.22 = bf16[64,4096]{1,0:T(8,128)(2,1)} all-gather(bf16[64,1024]{1,0:T(8,128)(2,1)S(1)} %get-tuple-element.157), channel_id=1, replica_groups=mesh['rep'=4,'row'=2,'col'=4] {'col'}, dimensions={1}, use_global_device_ids=true | all-gather | bytes 655360 | tf_op jit(solution)/shard_map/all_gather | solution.py:48
  480.1 0.6 dynamic-slice
  481.3 0.1 compare_select_fusion
  481.4 0.8 gather_fusion.2
  482.2 0.8 gather_fusion
  483.0 32.0 %all-reduce.3.cloned.1.call-done = f32[64,4096]{1,0:T(8,128)} async-done(((f32[64,4096]{1,0:T(8,128)}), f32[64,4096]{1,0:T(8,128)}) %all-reduce.3.cloned.1.call-update) | async-done | bytes 1048592 | tf_op jit(solution)/shard_map/psum | solution.py:52
  515.0 1.6 multiply_reduce_fusion
  516.6 4.9 psum.15
  521.5 0.1 fusion.4
  521.6 5.6 %all-reduce = f32[256]{0:T(256)S(1)} all-reduce(f32[256]{0:T(256)S(1)} %fusion.4), channel_id=1, replica_groups=mesh['rep'=4,'row'=2,'col'=4] {'rep'}, use_global_device_ids=true, to_apply=%add | all-reduce | flops 256 | bytes 2048
  527.2 0.8 gather_fusion.1
  528.0 0.6 select_multiply_fusion
  528.6 3.2 gather_fusion.3
  531.8 2.0 broadcast_select_fusion
  (46 shorter events, 0.7 us)
Async XLA Ops:
  8.0 1.0 copy-start
  12.4 45.9 %reduce-scatter.2.cloned.1.call-start = ((), (), s32[]{:S(2)}) async-start(), calls=%async_computation.3 | async-start | bytes 1310720 | tf_op jit(solution)/shard_map/while/body/eval_jaxpr/reduce_scatter | solution.py:40
  59.4 41.6 %reduce-scatter.2.cloned.1.call-start = ((), (), s32[]{:S(2)}) async-start(), calls=%async_computation.3 | async-start | bytes 1310720 | tf_op jit(solution)/shard_map/while/body/eval_jaxpr/reduce_scatter | solution.py:40
  102.1 41.6 %reduce-scatter.2.cloned.1.call-start = ((), (), s32[]{:S(2)}) async-start(), calls=%async_computation.3 | async-start | bytes 1310720 | tf_op jit(solution)/shard_map/while/body/eval_jaxpr/reduce_scatter | solution.py:40
  144.9 41.7 %reduce-scatter.2.cloned.1.call-start = ((), (), s32[]{:S(2)}) async-start(), calls=%async_computation.3 | async-start | bytes 1310720 | tf_op jit(solution)/shard_map/while/body/eval_jaxpr/reduce_scatter | solution.py:40
  187.6 41.6 %reduce-scatter.2.cloned.1.call-start = ((), (), s32[]{:S(2)}) async-start(), calls=%async_computation.3 | async-start | bytes 1310720 | tf_op jit(solution)/shard_map/while/body/eval_jaxpr/reduce_scatter | solution.py:40
  230.3 41.6 %reduce-scatter.2.cloned.1.call-start = ((), (), s32[]{:S(2)}) async-start(), calls=%async_computation.3 | async-start | bytes 1310720 | tf_op jit(solution)/shard_map/while/body/eval_jaxpr/reduce_scatter | solution.py:40
  273.1 41.6 %reduce-scatter.2.cloned.1.call-start = ((), (), s32[]{:S(2)}) async-start(), calls=%async_computation.3 | async-start | bytes 1310720 | tf_op jit(solution)/shard_map/while/body/eval_jaxpr/reduce_scatter | solution.py:40
  315.8 41.6 %reduce-scatter.2.cloned.1.call-start = ((), (), s32[]{:S(2)}) async-start(), calls=%async_computation.3 | async-start | bytes 1310720 | tf_op jit(solution)/shard_map/while/body/eval_jaxpr/reduce_scatter | solution.py:40
  358.6 41.6 %reduce-scatter.2.cloned.1.call-start = ((), (), s32[]{:S(2)}) async-start(), calls=%async_computation.3 | async-start | bytes 1310720 | tf_op jit(solution)/shard_map/while/body/eval_jaxpr/reduce_scatter | solution.py:40
  401.3 41.6 %reduce-scatter.2.cloned.1.call-start = ((), (), s32[]{:S(2)}) async-start(), calls=%async_computation.3 | async-start | bytes 1310720 | tf_op jit(solution)/shard_map/while/body/eval_jaxpr/reduce_scatter | solution.py:40
  444.1 36.0 %copy-start.2 = (s32[256]{0:T(256)S(1)}, s32[256]{0:T(256)}, u32[]{:S(2)}) copy-start(s32[256]{0:T(256)} %param.13) | copy-start | bytes 3076
  444.1 36.0 %copy-start.4 = (u32[32]{0:T(128)S(1)}, u32[32]{0:T(128)}, u32[]{:S(2)}) copy-start(u32[32]{0:T(128)} %constant.92) | copy-start | bytes 388
  444.1 37.2 %copy-start.3 = (s32[256]{0:T(256)S(1)}, s32[256]{0:T(256)}, u32[]{:S(2)}) copy-start(s32[256]{0:T(256)} %param.14) | copy-start | bytes 3076
  444.1 37.3 %copy-start.1 = (f32[256]{0:T(256)S(1)}, f32[256]{0:T(256)}, u32[]{:S(2)}) copy-start(f32[256]{0:T(256)} %param.15) | copy-start | bytes 3076
  444.1 70.9 %all-reduce.3.cloned.1.call-start = ((), (), s32[]{:S(2)}) async-start(), calls=%async_computation.1 | async-start | bytes 2097152 | tf_op jit(solution)/shard_map/psum | solution.py:52
  459.6 69.0 %all-gather.2.cloned.1.call-start = ((), (), s32[]{:S(2)}) async-start(), calls=%async_computation.2 | async-start | bytes 2621440 | tf_op jit(solution)/shard_map/all_gather | solution.py:49
Sparse Core Ops, SparseCore 0:
  29.5 28.7 reduce-scatter.1
  75.0 25.9 reduce-scatter.1
  117.7 25.9 reduce-scatter.1
  160.5 26.0 reduce-scatter.1
  203.2 25.9 reduce-scatter.1
  246.0 25.9 reduce-scatter.1
  288.7 25.9 reduce-scatter.1
  331.4 25.9 reduce-scatter.1
  374.2 25.9 reduce-scatter.1
  416.9 25.9 reduce-scatter.1
  480.2 21.6 all-gather.1
Sparse Core Ops, SparseCore 1:
  459.7 55.3 all-reduce.2
where the time goes:
time: 542 us; the launch traced here: 541 us
  waiting for transfers between devices  296 us (55%)
  matrix products  107 us (20%)
  blocking collectives  94.4 us (17%)
  other arithmetic  16 us (3%)
  between operations  15.9 us (3%)
  local copies, waits for them, and re-layouts  9.87 us (2%)
    reduce_scatter x10, waiting for transfers between devices, one_sweep(): fields = lax.psum_scatter(terms, 'col', scatter_dimension=1, tiled=True)  264 us
    dot_general x11, matrix products, partial_fields(): return jnp.dot(strided, coupling_block, preferred_element_type=jnp.float32)  107 us
    all_gather x11, blocking collectives, strided_of(): return lax.all_gather(spin_state, 'row', axis=1, tiled=True)  63.5 us
    psum x1, waiting for transfers between devices, per_device(): final_local = lax.psum(final_partial, 'col')  32 us
    all_gather x1, blocking collectives, per_device(): final_rows = lax.all_gather(final_pieces, 'col', axis=1, tiled=True)  20.4 us
    convert_element_type x10, other arithmetic, metropolis(): return jnp.where(flipped, -values, values).astype(jnp.bfloat16)  10.9 us
  transfers between devices with their start and end apart: 12, of which 11 were waited for; matrix products, arithmetic and copies ran while one was open for 1% of the time, Pallas kernels for 0%

commit v1 on v0

--- a/solution.py
+++ b/solution.py
@@ -49,7 +49,11 @@
     every_spins = lax.all_gather(final_rows, "rep", axis=0, tiled=True)
     final_partial = partial_fields(strided, coupling_block)
     row_values = final_rows.astype(jnp.float32)
-    final_local = lax.psum(final_partial, "col")
+    final_local = final_partial
+    for hop in (1, 2):
+        final_local = final_local + lax.ppermute(
+            final_local, "col", [(dev, dev ^ hop) for dev in range(4)]
+        )
     total_sum = lax.psum(jnp.sum(row_values * final_local, axis=1), "row")
     energy = -0.5 * total_sum
     every_energy = lax.all_gather(energy, "rep", axis=0, tiled=True)

time: 542 us -> 563 us (1.039)
  waiting for transfers between devices: 296 us -> 323 us
    ppermute x0 -> x2, waiting for transfers between devices: none -> 58.7 us  [per_device(): lax.ppermute(final_local, 'col', [(dev, dev ^ hop) for dev in range(4)])]
    psum x1 -> x0, waiting for transfers between devices: 32 us -> none  [per_device(): final_local = lax.psum(final_partial, 'col')]
  transfers between devices with their start and end apart: 12 -> 13, of which waited for: 11 -> 12; matrix products, arithmetic and copies ran while one was open for 1% -> 2% of each run, Pallas kernels for 0% -> 0%
where the time goes in v1:
time: 563 us; the launch traced here: 561 us
  waiting for transfers between devices  323 us (57%)
  matrix products  107 us (19%)
  blocking collectives  90.9 us (16%)
  between operations  16.3 us (3%)
  other arithmetic  13.8 us (2%)
  local copies, waits for them, and re-layouts  9.88 us (2%)
    reduce_scatter x10, waiting for transfers between devices, one_sweep(): fields = lax.psum_scatter(terms, 'col', scatter_dimension=1, tiled=True)  264 us
    dot_general x11, matrix products, partial_fields(): return jnp.dot(strided, coupling_block, preferred_element_type=jnp.float32)  107 us
    all_gather x11, blocking collectives, strided_of(): return lax.all_gather(spin_state, 'row', axis=1, tiled=True)  63.6 us
    ppermute x2, waiting for transfers between devices, per_device(): lax.ppermute(final_local, 'col', [(dev, dev ^ hop) for dev in range(4)])  58.7 us
    all_gather x1, blocking collectives, per_device(): final_rows = lax.all_gather(final_pieces, 'col', axis=1, tiled=True)  16.7 us
  transfers between devices with their start and end apart: 13, of which 12 were waited for; matrix products, arithmetic and copies ran while one was open for 2% of the time, Pallas kernels for 0%

profile of v1, /device:TPU:0, one launch (start us, length us, event | category | flops | bytes accessed | tf_op | source)
XLA Modules:
  0.0 561.4 jit_solution(971610161679469433)
XLA Ops:
  8.0 1.0 copy-done
  9.1 0.7 dynamic_slice.28
  9.8 1.9 constant_dynamic-slice_fusion
  11.7 0.8 convert_bitcast_fusion
  12.4 431.6 %while.15 = (s32[]{:T(128)}, bf16[64,1024]{1,0:T(8,128)(2,1)S(1)}, s32[1024]{0:T(1024)S(1)}, f32[64,1]{0,1:T(1,128)S(1)}, bf16[2048,4096]{1,0:T(8,128)(2,1)}, /*...) while((s32[]{:T(128)}, bf16[64,1024]{1,0:T(8,128)(2,1)S(1)}, s32[1024]{0:T(1024)S(1)}, ...), condition=%wide.region_2.3_spmd, body=%wide.region_0.2_spmd.sunk | while | flops 1074332672 | bytes 23206348 | solution.py:46
  12.4 7.1 %all_gather.27 = bf16[64,2048]{1,0:T(8,128)(2,1)S(1)} all-gather(bf16[64,1024]{1,0:T(8,128)(2,1)S(1)} %get-tuple-element.221), channel_id=1, replica_groups=mesh['rep'=4,'row'=2,'col'=4] {'row'}, dimensions={1}, use_global_device_ids=true | all-gather | bytes 393216 | tf_op jit(solution)/shard_map/while/body/eval_jaxpr/all_gather | solution.py:36
  19.6 9.8 %fusion.17 = f32[64,4096]{1,0:T(8,128)} fusion(bf16[64,2048]{1,0:T(8,128)(2,1)S(1)} %all_gather.27, bf16[2048,4096]{1,0:T(8,128)(2,1)} %get-tuple-element.233), kind=kOutput, calls=%fused_computation.24.clone.1 | convolution fusion | flops 1073741824 | bytes 18087936 | tf_op jit(solution)/shard_map/while/body/eval_jaxpr/dot_general | solution.py:19
  29.4 28.9 %reduce-scatter.2.cloned.1.call-done = f32[64,1024]{1,0:T(8,128)} async-done(((f32[64,4096]{1,0:T(8,128)}), f32[64,1024]{1,0:T(8,128)}) %reduce-scatter.2.cloned.1.call-update) | async-done | bytes 262160 | tf_op jit(solution)/shard_map/while/body/eval_jaxpr/reduce_scatter | solution.py:40
  58.3 1.1 fusion.18
  59.5 5.6 %all_gather.27 = bf16[64,2048]{1,0:T(8,128)(2,1)S(1)} all-gather(bf16[64,1024]{1,0:T(8,128)(2,1)S(1)} %get-tuple-element.221), channel_id=1, replica_groups=mesh['rep'=4,'row'=2,'col'=4] {'row'}, dimensions={1}, use_global_device_ids=true | all-gather | bytes 393216 | tf_op jit(solution)/shard_map/while/body/eval_jaxpr/all_gather | solution.py:36
  65.1 9.8 %fusion.17 = f32[64,4096]{1,0:T(8,128)} fusion(bf16[64,2048]{1,0:T(8,128)(2,1)S(1)} %all_gather.27, bf16[2048,4096]{1,0:T(8,128)(2,1)} %get-tuple-element.233), kind=kOutput, calls=%fused_computation.24.clone.1 | convolution fusion | flops 1073741824 | bytes 18087936 | tf_op jit(solution)/shard_map/while/body/eval_jaxpr/dot_general | solution.py:19
  74.9 26.1 %reduce-scatter.2.cloned.1.call-done = f32[64,1024]{1,0:T(8,128)} async-done(((f32[64,4096]{1,0:T(8,128)}), f32[64,1024]{1,0:T(8,128)}) %reduce-scatter.2.cloned.1.call-update) | async-done | bytes 262160 | tf_op jit(solution)/shard_map/while/body/eval_jaxpr/reduce_scatter | solution.py:40
  101.0 1.1 fusion.18
  102.2 5.6 %all_gather.27 = bf16[64,2048]{1,0:T(8,128)(2,1)S(1)} all-gather(bf16[64,1024]{1,0:T(8,128)(2,1)S(1)} %get-tuple-element.221), channel_id=1, replica_groups=mesh['rep'=4,'row'=2,'col'=4] {'row'}, dimensions={1}, use_global_device_ids=true | all-gather | bytes 393216 | tf_op jit(solution)/shard_map/while/body/eval_jaxpr/all_gather | solution.py:36
  107.8 9.8 %fusion.17 = f32[64,4096]{1,0:T(8,128)} fusion(bf16[64,2048]{1,0:T(8,128)(2,1)S(1)} %all_gather.27, bf16[2048,4096]{1,0:T(8,128)(2,1)} %get-tuple-element.233), kind=kOutput, calls=%fused_computation.24.clone.1 | convolution fusion | flops 1073741824 | bytes 18087936 | tf_op jit(solution)/shard_map/while/body/eval_jaxpr/dot_general | solution.py:19
  117.6 26.2 %reduce-scatter.2.cloned.1.call-done = f32[64,1024]{1,0:T(8,128)} async-done(((f32[64,4096]{1,0:T(8,128)}), f32[64,1024]{1,0:T(8,128)}) %reduce-scatter.2.cloned.1.call-update) | async-done | bytes 262160 | tf_op jit(solution)/shard_map/while/body/eval_jaxpr/reduce_scatter | solution.py:40
  143.8 1.1 fusion.18
  144.9 5.6 %all_gather.27 = bf16[64,2048]{1,0:T(8,128)(2,1)S(1)} all-gather(bf16[64,1024]{1,0:T(8,128)(2,1)S(1)} %get-tuple-element.221), channel_id=1, replica_groups=mesh['rep'=4,'row'=2,'col'=4] {'row'}, dimensions={1}, use_global_device_ids=true | all-gather | bytes 393216 | tf_op jit(solution)/shard_map/while/body/eval_jaxpr/all_gather | solution.py:36
  150.6 9.8 %fusion.17 = f32[64,4096]{1,0:T(8,128)} fusion(bf16[64,2048]{1,0:T(8,128)(2,1)S(1)} %all_gather.27, bf16[2048,4096]{1,0:T(8,128)(2,1)} %get-tuple-element.233), kind=kOutput, calls=%fused_computation.24.clone.1 | convolution fusion | flops 1073741824 | bytes 18087936 | tf_op jit(solution)/shard_map/while/body/eval_jaxpr/dot_general | solution.py:19
  160.4 26.1 %reduce-scatter.2.cloned.1.call-done = f32[64,1024]{1,0:T(8,128)} async-done(((f32[64,4096]{1,0:T(8,128)}), f32[64,1024]{1,0:T(8,128)}) %reduce-scatter.2.cloned.1.call-update) | async-done | bytes 262160 | tf_op jit(solution)/shard_map/while/body/eval_jaxpr/reduce_scatter | solution.py:40
  186.5 1.1 fusion.18
  187.7 5.6 %all_gather.27 = bf16[64,2048]{1,0:T(8,128)(2,1)S(1)} all-gather(bf16[64,1024]{1,0:T(8,128)(2,1)S(1)} %get-tuple-element.221), channel_id=1, replica_groups=mesh['rep'=4,'row'=2,'col'=4] {'row'}, dimensions={1}, use_global_device_ids=true | all-gather | bytes 393216 | tf_op jit(solution)/shard_map/while/body/eval_jaxpr/all_gather | solution.py:36
  193.3 9.8 %fusion.17 = f32[64,4096]{1,0:T(8,128)} fusion(bf16[64,2048]{1,0:T(8,128)(2,1)S(1)} %all_gather.27, bf16[2048,4096]{1,0:T(8,128)(2,1)} %get-tuple-element.233), kind=kOutput, calls=%fused_computation.24.clone.1 | convolution fusion | flops 1073741824 | bytes 18087936 | tf_op jit(solution)/shard_map/while/body/eval_jaxpr/dot_general | solution.py:19
  203.1 26.1 %reduce-scatter.2.cloned.1.call-done = f32[64,1024]{1,0:T(8,128)} async-done(((f32[64,4096]{1,0:T(8,128)}), f32[64,1024]{1,0:T(8,128)}) %reduce-scatter.2.cloned.1.call-update) | async-done | bytes 262160 | tf_op jit(solution)/shard_map/while/body/eval_jaxpr/reduce_scatter | solution.py:40
  229.2 1.1 fusion.18
  230.4 5.6 %all_gather.27 = bf16[64,2048]{1,0:T(8,128)(2,1)S(1)} all-gather(bf16[64,1024]{1,0:T(8,128)(2,1)S(1)} %get-tuple-element.221), channel_id=1, replica_groups=mesh['rep'=4,'row'=2,'col'=4] {'row'}, dimensions={1}, use_global_device_ids=true | all-gather | bytes 393216 | tf_op jit(solution)/shard_map/while/body/eval_jaxpr/all_gather | solution.py:36
  236.0 9.8 %fusion.17 = f32[64,4096]{1,0:T(8,128)} fusion(bf16[64,2048]{1,0:T(8,128)(2,1)S(1)} %all_gather.27, bf16[2048,4096]{1,0:T(8,128)(2,1)} %get-tuple-element.233), kind=kOutput, calls=%fused_computation.24.clone.1 | convolution fusion | flops 1073741824 | bytes 18087936 | tf_op jit(solution)/shard_map/while/body/eval_jaxpr/dot_general | solution.py:19
  245.8 26.1 %reduce-scatter.2.cloned.1.call-done = f32[64,1024]{1,0:T(8,128)} async-done(((f32[64,4096]{1,0:T(8,128)}), f32[64,1024]{1,0:T(8,128)}) %reduce-scatter.2.cloned.1.call-update) | async-done | bytes 262160 | tf_op jit(solution)/shard_map/while/body/eval_jaxpr/reduce_scatter | solution.py:40
  272.0 1.1 fusion.18
  273.1 5.6 %all_gather.27 = bf16[64,2048]{1,0:T(8,128)(2,1)S(1)} all-gather(bf16[64,1024]{1,0:T(8,128)(2,1)S(1)} %get-tuple-element.221), channel_id=1, replica_groups=mesh['rep'=4,'row'=2,'col'=4] {'row'}, dimensions={1}, use_global_device_ids=true | all-gather | bytes 393216 | tf_op jit(solution)/shard_map/while/body/eval_jaxpr/all_gather | solution.py:36
  278.8 9.8 %fusion.17 = f32[64,4096]{1,0:T(8,128)} fusion(bf16[64,2048]{1,0:T(8,128)(2,1)S(1)} %all_gather.27, bf16[2048,4096]{1,0:T(8,128)(2,1)} %get-tuple-element.233), kind=kOutput, calls=%fused_computation.24.clone.1 | convolution fusion | flops 1073741824 | bytes 18087936 | tf_op jit(solution)/shard_map/while/body/eval_jaxpr/dot_general | solution.py:19
  288.6 26.1 %reduce-scatter.2.cloned.1.call-done = f32[64,1024]{1,0:T(8,128)} async-done(((f32[64,4096]{1,0:T(8,128)}), f32[64,1024]{1,0:T(8,128)}) %reduce-scatter.2.cloned.1.call-update) | async-done | bytes 262160 | tf_op jit(solution)/shard_map/while/body/eval_jaxpr/reduce_scatter | solution.py:40
  314.7 1.1 fusion.18
  315.9 5.6 %all_gather.27 = bf16[64,2048]{1,0:T(8,128)(2,1)S(1)} all-gather(bf16[64,1024]{1,0:T(8,128)(2,1)S(1)} %get-tuple-element.221), channel_id=1, replica_groups=mesh['rep'=4,'row'=2,'col'=4] {'row'}, dimensions={1}, use_global_device_ids=true | all-gather | bytes 393216 | tf_op jit(solution)/shard_map/while/body/eval_jaxpr/all_gather | solution.py:36
  321.5 9.8 %fusion.17 = f32[64,4096]{1,0:T(8,128)} fusion(bf16[64,2048]{1,0:T(8,128)(2,1)S(1)} %all_gather.27, bf16[2048,4096]{1,0:T(8,128)(2,1)} %get-tuple-element.233), kind=kOutput, calls=%fused_computation.24.clone.1 | convolution fusion | flops 1073741824 | bytes 18087936 | tf_op jit(solution)/shard_map/while/body/eval_jaxpr/dot_general | solution.py:19
  331.3 26.1 %reduce-scatter.2.cloned.1.call-done = f32[64,1024]{1,0:T(8,128)} async-done(((f32[64,4096]{1,0:T(8,128)}), f32[64,1024]{1,0:T(8,128)}) %reduce-scatter.2.cloned.1.call-update) | async-done | bytes 262160 | tf_op jit(solution)/shard_map/while/body/eval_jaxpr/reduce_scatter | solution.py:40
  357.5 1.1 fusion.18
  358.6 5.6 %all_gather.27 = bf16[64,2048]{1,0:T(8,128)(2,1)S(1)} all-gather(bf16[64,1024]{1,0:T(8,128)(2,1)S(1)} %get-tuple-element.221), channel_id=1, replica_groups=mesh['rep'=4,'row'=2,'col'=4] {'row'}, dimensions={1}, use_global_device_ids=true | all-gather | bytes 393216 | tf_op jit(solution)/shard_map/while/body/eval_jaxpr/all_gather | solution.py:36
  364.3 9.8 %fusion.17 = f32[64,4096]{1,0:T(8,128)} fusion(bf16[64,2048]{1,0:T(8,128)(2,1)S(1)} %all_gather.27, bf16[2048,4096]{1,0:T(8,128)(2,1)} %get-tuple-element.233), kind=kOutput, calls=%fused_computation.24.clone.1 | convolution fusion | flops 1073741824 | bytes 18087936 | tf_op jit(solution)/shard_map/while/body/eval_jaxpr/dot_general | solution.py:19
  374.1 26.1 %reduce-scatter.2.cloned.1.call-done = f32[64,1024]{1,0:T(8,128)} async-done(((f32[64,4096]{1,0:T(8,128)}), f32[64,1024]{1,0:T(8,128)}) %reduce-scatter.2.cloned.1.call-update) | async-done | bytes 262160 | tf_op jit(solution)/shard_map/while/body/eval_jaxpr/reduce_scatter | solution.py:40
  400.2 1.1 fusion.18
  401.4 5.6 %all_gather.27 = bf16[64,2048]{1,0:T(8,128)(2,1)S(1)} all-gather(bf16[64,1024]{1,0:T(8,128)(2,1)S(1)} %get-tuple-element.221), channel_id=1, replica_groups=mesh['rep'=4,'row'=2,'col'=4] {'row'}, dimensions={1}, use_global_device_ids=true | all-gather | bytes 393216 | tf_op jit(solution)/shard_map/while/body/eval_jaxpr/all_gather | solution.py:36
  407.0 9.8 %fusion.17 = f32[64,4096]{1,0:T(8,128)} fusion(bf16[64,2048]{1,0:T(8,128)(2,1)S(1)} %all_gather.27, bf16[2048,4096]{1,0:T(8,128)(2,1)} %get-tuple-element.233), kind=kOutput, calls=%fused_computation.24.clone.1 | convolution fusion | flops 1073741824 | bytes 18087936 | tf_op jit(solution)/shard_map/while/body/eval_jaxpr/dot_general | solution.py:19
  416.8 26.1 %reduce-scatter.2.cloned.1.call-done = f32[64,1024]{1,0:T(8,128)} async-done(((f32[64,4096]{1,0:T(8,128)}), f32[64,1024]{1,0:T(8,128)}) %reduce-scatter.2.cloned.1.call-update) | async-done | bytes 262160 | tf_op jit(solution)/shard_map/while/body/eval_jaxpr/reduce_scatter | solution.py:40
  442.9 1.1 fusion.18
  444.2 16.7 %all_gather.22 = bf16[64,4096]{1,0:T(8,128)(2,1)} all-gather(bf16[64,1024]{1,0:T(8,128)(2,1)S(1)} %get-tuple-element.157), channel_id=1, replica_groups=mesh['rep'=4,'row'=2,'col'=4] {'col'}, dimensions={1}, use_global_device_ids=true | all-gather | bytes 655360 | tf_op jit(solution)/shard_map/all_gather | solution.py:48
  460.8 5.8 %all_gather.23 = bf16[64,2048]{1,0:T(8,128)(2,1)S(1)} all-gather(bf16[64,1024]{1,0:T(8,128)(2,1)S(1)} %get-tuple-element.157), channel_id=1, replica_groups=mesh['rep'=4,'row'=2,'col'=4] {'row'}, dimensions={1}, use_global_device_ids=true | all-gather | bytes 393216 | tf_op jit(solution)/shard_map/all_gather | solution.py:36
  466.6 8.9 %fusion.6 = f32[64,4096]{1,0:T(8,128)S(1)} fusion(bf16[64,2048]{1,0:T(8,128)(2,1)S(1)} %all_gather.23, bf16[2048,4096]{1,0:T(8,128)(2,1)} %get-tuple-element.240), kind=kOutput, calls=%fused_computation.25 | convolution fusion | flops 1073741824 | bytes 18087936 | tf_op jit(solution)/shard_map/dot_general | solution.py:19
  475.5 0.1 collective-permute-start
  475.6 22.9 %collective-permute-done = f32[64,4096]{1,0:T(8,128)S(1)} collective-permute-done((f32[64,4096]{1,0:T(8,128)S(1)}, f32[64,4096]{1,0:T(8,128)S(1)}, u32[]{:S(2)}, u32[]{:S(2)}) %collective-permute-start) | collective-permute-done | bytes 1048608 | tf_op jit(solution)/shard_map/ppermute | solution.py:54
  498.5 0.1 add.78
  498.8 0.6 dynamic-slice
  500.0 0.1 compare_select_fusion
  500.1 0.8 gather_fusion.2
  500.9 0.8 gather_fusion
  501.7 35.8 %collective-permute-done.1 = f32[64,4096]{1,0:T(8,128)S(1)} collective-permute-done((f32[64,4096]{1,0:T(8,128)S(1)}, f32[64,4096]{1,0:T(8,128)S(1)}, u32[]{:S(2)}, u32[]{:S(2)}) %collective-permute-start.1) | collective-permute-done | bytes 1048608 | tf_op jit(solution)/shard_map/ppermute | solution.py:54
  537.5 0.3 multiply_reduce_fusion
  537.8 4.9 psum.7
  542.7 0.1 fusion.4
  542.8 5.6 %all-reduce = f32[256]{0:T(256)S(1)} all-reduce(f32[256]{0:T(256)S(1)} %fusion.4), channel_id=1, replica_groups=mesh['rep'=4,'row'=2,'col'=4] {'rep'}, use_global_device_ids=true, to_apply=%add | all-reduce | flops 256 | bytes 2048
  548.5 0.8 gather_fusion.1
  549.3 0.6 select_multiply_fusion
  549.8 3.2 gather_fusion.3
  553.1 0.9 broadcast_select_fusion
  (50 shorter events, 0.8 us)
Async XLA Ops:
  8.0 1.0 copy-start
  12.4 45.9 %reduce-scatter.2.cloned.1.call-start = ((), (), s32[]{:S(2)}) async-start(), calls=%async_computation.2 | async-start | bytes 1310720 | tf_op jit(solution)/shard_map/while/body/eval_jaxpr/reduce_scatter | solution.py:40
  59.4 41.6 %reduce-scatter.2.cloned.1.call-start = ((), (), s32[]{:S(2)}) async-start(), calls=%async_computation.2 | async-start | bytes 1310720 | tf_op jit(solution)/shard_map/while/body/eval_jaxpr/reduce_scatter | solution.py:40
  102.1 41.7 %reduce-scatter.2.cloned.1.call-start = ((), (), s32[]{:S(2)}) async-start(), calls=%async_computation.2 | async-start | bytes 1310720 | tf_op jit(solution)/shard_map/while/body/eval_jaxpr/reduce_scatter | solution.py:40
  144.9 41.6 %reduce-scatter.2.cloned.1.call-start = ((), (), s32[]{:S(2)}) async-start(), calls=%async_computation.2 | async-start | bytes 1310720 | tf_op jit(solution)/shard_map/while/body/eval_jaxpr/reduce_scatter | solution.py:40
  187.6 41.6 %reduce-scatter.2.cloned.1.call-start = ((), (), s32[]{:S(2)}) async-start(), calls=%async_computation.2 | async-start | bytes 1310720 | tf_op jit(solution)/shard_map/while/body/eval_jaxpr/reduce_scatter | solution.py:40
  230.3 41.6 %reduce-scatter.2.cloned.1.call-start = ((), (), s32[]{:S(2)}) async-start(), calls=%async_computation.2 | async-start | bytes 1310720 | tf_op jit(solution)/shard_map/while/body/eval_jaxpr/reduce_scatter | solution.py:40
  273.1 41.6 %reduce-scatter.2.cloned.1.call-start = ((), (), s32[]{:S(2)}) async-start(), calls=%async_computation.2 | async-start | bytes 1310720 | tf_op jit(solution)/shard_map/while/body/eval_jaxpr/reduce_scatter | solution.py:40
  315.8 41.6 %reduce-scatter.2.cloned.1.call-start = ((), (), s32[]{:S(2)}) async-start(), calls=%async_computation.2 | async-start | bytes 1310720 | tf_op jit(solution)/shard_map/while/body/eval_jaxpr/reduce_scatter | solution.py:40
  358.6 41.6 %reduce-scatter.2.cloned.1.call-start = ((), (), s32[]{:S(2)}) async-start(), calls=%async_computation.2 | async-start | bytes 1310720 | tf_op jit(solution)/shard_map/while/body/eval_jaxpr/reduce_scatter | solution.py:40
  401.3 41.6 %reduce-scatter.2.cloned.1.call-start = ((), (), s32[]{:S(2)}) async-start(), calls=%async_computation.2 | async-start | bytes 1310720 | tf_op jit(solution)/shard_map/while/body/eval_jaxpr/reduce_scatter | solution.py:40
  444.0 54.7 %copy-start.3 = (s32[256]{0:T(256)S(1)}, s32[256]{0:T(256)}, u32[]{:S(2)}) copy-start(s32[256]{0:T(256)} %param.13) | copy-start | bytes 3076
  444.1 54.7 %copy-start.5 = (u32[32]{0:T(128)S(1)}, u32[32]{0:T(128)}, u32[]{:S(2)}) copy-start(u32[32]{0:T(128)} %constant.92) | copy-start | bytes 388
  444.1 55.9 %copy-start.4 = (s32[256]{0:T(256)S(1)}, s32[256]{0:T(256)}, u32[]{:S(2)}) copy-start(s32[256]{0:T(256)} %param.14) | copy-start | bytes 3076
  444.1 56.0 %copy-start.1 = (f32[256]{0:T(256)S(1)}, f32[256]{0:T(256)}, u32[]{:S(2)}) copy-start(f32[256]{0:T(256)} %param.15) | copy-start | bytes 3076
  444.1 105.7 %all-gather.2.cloned.1.call-start = ((), (), s32[]{:S(2)}) async-start(), calls=%async_computation.1 | async-start | bytes 2621440 | tf_op jit(solution)/shard_map/all_gather | solution.py:49
  460.8 76.7 %copy-start.2 = (bf16[64,4096]{1,0:T(8,128)(2,1)S(1)}, bf16[64,4096]{1,0:T(8,128)(2,1)}, u32[]{:S(2)}) copy-start(bf16[64,4096]{1,0:T(8,128)(2,1)} %all_gather.22) | copy-start | bytes 1572868
  475.5 23.0 %collective-permute-start = (f32[64,4096]{1,0:T(8,128)S(1)}, f32[64,4096]{1,0:T(8,128)S(1)}, u32[]{:S(2)}, u32[]{:S(2)}) collective-permute-start(f32[64,4096]{1,0:T(8,128)S(1)} %fusion.6), channel_id=1, source_target_pairs={{0,1},{1,0},{2,3},{3,2},{4,5},{5,4},{6,7},{7,6},{8,9},{9,8},{10,11... | collective-permute-start | bytes 3145736 | tf_op jit(solution)/shard_map/ppermute | solution.py:54
  498.7 38.9 %collective-permute-start.1 = (f32[64,4096]{1,0:T(8,128)S(1)}, f32[64,4096]{1,0:T(8,128)S(1)}, u32[]{:S(2)}, u32[]{:S(2)}) collective-permute-start(f32[64,4096]{1,0:T(8,128)S(1)} %add.78), channel_id=1, source_target_pairs={{0,2},{1,3},{2,0},{3,1},{4,6},{5,7},{6,4},{7,5},{8,10},{9,11},{10,... | collective-permute-start | bytes 3145736 | tf_op jit(solution)/shard_map/ppermute | solution.py:54
Sparse Core Ops, SparseCore 0:
  29.5 28.7 reduce-scatter.1
  75.0 25.9 reduce-scatter.1
  117.7 26.0 reduce-scatter.1
  160.5 25.9 reduce-scatter.1
  203.2 25.9 reduce-scatter.1
  245.9 25.9 reduce-scatter.1
  288.7 25.9 reduce-scatter.1
  331.4 25.9 reduce-scatter.1
  374.2 25.9 reduce-scatter.1
  416.9 25.9 reduce-scatter.1
Sparse Core Ops, SparseCore 1:
  460.9 20.6 all-gather.1
